TPU v7x, 32 devices: a 4x4x1 block of a 4x4x8 slice. The times are simulated.
32 devices in a mesh: dp: 1 (over z), tp: 32 (over x, y, core).
Axes of the slice: x: 4, y: 4, z: 1, core: 2. Of those that a mesh axis runs over, the one named last changes fastest.
The devices are a block of a 4x4x8 slice.
Arguments:
- x: bfloat16 [7168, 5120], P(('dp', 'tp'))
- w_gate: bfloat16 [5120, 16384], P(None, 'tp')
- w_up: bfloat16 [5120, 16384], P(None, 'tp')
- w_down: bfloat16 [16384, 5120], P('tp')
Outputs:
- output: bfloat16 [7168, 5120], P(('dp', 'tp'))
All inputs are finite; a program needn't handle non-finite values.
Results may differ from a plain program's by a relative error of at most 0.016.
Values are sent between devices in bfloat16 or wider.
A program may use at most 768 MiB of HBM per device.

v0:
```python
import jax
import jax.numpy as jnp
from jax import lax
from jax.sharding import PartitionSpec as P


def solution(mesh):
    def step(x, w_gate, w_up, w_down):
        rows = lax.all_gather(x, "tp", axis=0, tiled=True)
        gate = jnp.dot(rows, w_gate, preferred_element_type=jnp.float32)
        up = jnp.dot(rows, w_up, preferred_element_type=jnp.float32)
        hidden = (jax.nn.silu(gate) * up).astype(jnp.bfloat16)
        term = jnp.dot(hidden, w_down, preferred_element_type=jnp.float32).astype(jnp.bfloat16)
        return lax.psum_scatter(term, "tp", scatter_dimension=0, tiled=True)

    return jax.shard_map(
        step,
        mesh=mesh,
        in_specs=(P(("dp", "tp"), None), P(None, "tp"), P(None, "tp"), P("tp", None)),
        out_specs=P(("dp", "tp"), None),
        check_vma=False,
    )
```

profile of v0, /device:TPU:97, one launch (start us, length us, event | category | flops | bytes accessed | tf_op | source)
XLA Modules:
  0.0 678.9 jit_solution(5415587461733762631)
XLA Ops:
  6.5 0.0 all-gather.2.cloned.1.call-start
  6.6 0.7 all-gather.2.cloned.1.call-update
  7.3 0.1 reduce-scatter.4.cloned.1.call-start
  7.4 218.6 %all-gather.2.cloned.1.call-done = bf16[7168,5120]{1,0:T(8,128)(2,1)} async-done(((bf16[224,5120]{1,0:T(8,128)(2,1)}), bf16[7168,5120]{1,0:T(8,128)(2,1)}) %all-gather.2.cloned.1.call-update) | async-done | bytes 73400336 | tf_op jit(solution)/shard_map/all_gather | solution.py:9
  226.0 45.8 %fusion.1 = f32[7168,512]{1,0:T(8,128)} fusion(bf16[7168,5120]{1,0:T(8,128)(2,1)} %all-gather.2.cloned.1.call-done, bf16[5120,512]{1,0:T(8,128)(2,1)} %param.5), kind=kOutput, calls=%fused_computation.3 | convolution fusion | flops 37580963840 | bytes 93323264 | tf_op jit(solution)/shard_map/dot_general | solution.py:10
  271.7 51.3 %multiply_convert_fusion.clone.4 = bf16[7168,512]{1,0:T(8,128)(2,1)} fusion(f32[7168,512]{1,0:T(8,128)} %fusion.1, bf16[7168,5120]{1,0:T(8,128)(2,1)} %all-gather.2.cloned.1.call-done, bf16[5120,512]{1,0:T(8,128)(2,1)} %param.6), kind=kOutput, calls=%fused_computation.1.clone.clone.clone.1 | convolution fusion | flops 37602983936 | bytes 100663296 | tf_op jit(solution)/shard_map/dot_general | solution.py:11
  323.0 46.6 %convolution_convert_fusion = bf16[7168,5120]{1,0:T(8,128)(2,1)} fusion(bf16[512,5120]{1,0:T(8,128)(2,1)} %param.7, bf16[7168,512]{1,0:T(8,128)(2,1)} %multiply_convert_fusion.clone.4), kind=kOutput, calls=%fused_computation | convolution fusion | flops 37617664000 | bytes 85983232 | tf_op jit(solution)/shard_map/dot_general | solution.py:13
  369.6 0.1 reduce-scatter.4.cloned.1.call-update
  369.7 302.3 %reduce-scatter.4.cloned.1.call-done = bf16[224,5120]{1,0:T(8,128)(2,1)} async-done(((bf16[7168,5120]{1,0:T(8,128)(2,1)}), bf16[224,5120]{1,0:T(8,128)(2,1)}) %reduce-scatter.4.cloned.1.call-update) | async-done | bytes 2293776
Async XLA Ops:
  6.5 219.4 %all-gather.2.cloned.1.call-start = ((), (), s32[]{:S(2)}) async-start(), calls=%async_computation.1 | async-start | bytes 75694080 | tf_op jit(solution)/shard_map/all_gather | solution.py:9
  7.3 664.7 %reduce-scatter.4.cloned.1.call-start = ((), (), s32[]{:S(2)}) async-start(), calls=%async_computation.2 | async-start | bytes 75694080
Sparse Core Ops, SparseCore 0:
  9.4 216.4 all-gather.1
  369.8 302.1 reduce-scatter.3
where the time goes:
time: 679 us
  waiting for transfers between devices  522 us (77%)
  matrix products  144 us (21%)
  between operations  13.4 us (2%)
    unnamed x3, waiting for transfers between devices  303 us
    all_gather x1, waiting for transfers between devices, step(): rows = lax.all_gather(x, 'tp', axis=0, tiled=True)  219 us
    dot_general x1, matrix products, step(): up = jnp.dot(rows, w_up, preferred_element_type=jnp.float32)  51.3 us
    dot_general x1, matrix products, step(): jnp.dot(hidden, w_down, preferred_element_type=jnp.float32)  46.6 us
    dot_general x1, matrix products, step(): gate = jnp.dot(rows, w_gate, preferred_element_type=jnp.float32)  45.8 us
  transfers between devices with their start and end apart: 2, of which 2 were waited for; matrix products, arithmetic and copies ran while one was open for 0% of the time, Pallas kernels for 0%

commit v1 on v0

v1 whole, which is shorter than its diff:
```python
import functools
import math

import jax
import jax.numpy as jnp
from jax import lax
from jax.experimental import pallas as pl
from jax.experimental.pallas import tpu as pltpu
from jax.sharding import PartitionSpec as P

MESH = pl.DeviceIdType.MESH
F32, BF16 = jnp.float32, jnp.bfloat16
TU = 128
CW = 256


def kernel(side, x_ref, wg_ref, wu_ref, wd_ref, y_ref, G, U, D,
           xa, hid, rf, rn, rx, gt, wt, sf, sn, sx, own, yo,
           ssem, rsem, lsem, gsem, wsem, fs, fr, ns, nr, xs, xr, ysem):
    t = lax.axis_index("tp")
    core, row, col = t % 2, (t // 2) % side, t // (2 * side)

    def peer(dx, dy, dc):
        return (((col + dx + side) % side) * side + (row + dy + side) % side) * 2 + (core + dc) % 2

    XP, XM, X2 = peer(1, 0, 0), peer(-1, 0, 0), peer(2, 0, 0)
    YP, YM, CC = peer(0, 1, 0), peer(0, -1, 0), peer(0, 0, 1)

    R, d = x_ref.shape
    h = R // 2
    units = wg_ref.shape[1]
    k = units // 2
    NJ = d // CW

    barrier = pltpu.get_barrier_semaphore()
    for p in (XP, XM, X2, YP, YM, CC):
        pl.semaphore_signal(barrier, inc=1, device_id={"tp": p}, device_id_type=MESH)
    pl.semaphore_wait(barrier, 6)

    def remote(src, dst, s, r, to):
        return pltpu.make_async_remote_copy(
            src_ref=src, dst_ref=dst, send_sem=s, recv_sem=r, device_id={"tp": to}, device_id_type=MESH)

    jobs = {}

    def job(name, src, dst, to):
        i = len(jobs)
        jobs[name] = remote(src, dst, ssem.at[i], rsem.at[i], to)

    job("ax", x_ref, xa.at[0, pl.ds(R, R)], X2)
    job("r1", x_ref, xa.at[1, pl.ds(0, R)], YP)
    job("l1", x_ref, xa.at[2, pl.ds(0, R)], YM)
    job("r1x", xa.at[0, pl.ds(R, R)], xa.at[1, pl.ds(R, R)], YP)
    job("l1x", xa.at[0, pl.ds(R, R)], xa.at[2, pl.ds(R, R)], YM)
    job("d2p", xa.at[1, pl.ds(0, h)], xa.at[3, pl.ds(0, h)], YP)
    job("d2m", xa.at[2, pl.ds(h, h)], xa.at[3, pl.ds(h, h)], YM)
    job("d2xp", xa.at[1, pl.ds(R, h)], xa.at[3, pl.ds(R, h)], YP)
    job("d2xm", xa.at[2, pl.ds(R + h, h)], xa.at[3, pl.ds(R + h, h)], YM)
    job("mg", wg_ref, G.at[0], CC)
    job("mu", wu_ref, U.at[0], CC)
    job("md", wd_ref, D.at[0], CC)
    for i, to in ((0, XP), (1, XM)):
        lo = pl.ds(i * k, k)
        job(f"ng{i}", wg_ref.at[:, lo], G.at[1, :, lo], to)
        job(f"nu{i}", wu_ref.at[:, lo], U.at[1, :, lo], to)
        for q in range(2):
            rows = pl.ds(i * k + q * (k // 2), k // 2)
            job(f"nd{i}{q}", wd_ref.at[rows], D.at[1, rows], to)
            job(f"qd{i}{q}", D.at[1, rows], D.at[2, rows], CC)
        job(f"qg{i}", G.at[1, :, lo], G.at[2, :, lo], CC)
        job(f"qu{i}", U.at[1, :, lo], U.at[2, :, lo], CC)

    def start(*names):
        for a in names:
            jobs[a].start()

    def got(*names):
        for a in names:
            jobs[a].wait_recv()

    mine = pltpu.make_async_copy(x_ref, xa.at[0, pl.ds(0, R)], lsem)
    mine.start()
    start("ax", "r1", "l1", "mg", "mu")
    start("ng0", "ng1", "nu0", "nu1", "nd00", "nd10", "nd01", "nd11", "md")

    per = units // TU

    def tile(tt, slot, act):
        kind = tt // per
        cols = pl.ds(pl.multiple_of((tt % per) * TU, TU), TU)
        for i, (w, b) in enumerate(((wg_ref, G), (wu_ref, U))):
            dst = gt.at[slot, :, pl.ds(i * TU, TU)]
            if act == "wait":
                pltpu.make_async_copy(w.at[:, pl.ds(0, TU)], dst, gsem.at[slot, i]).wait()
                continue

            @pl.when(kind == 0)
            def _():
                pltpu.make_async_copy(w.at[:, cols], dst, gsem.at[slot, i]).start()

            @pl.when(kind > 0)
            def _():
                pltpu.make_async_copy(b.at[jnp.maximum(kind - 1, 0), :, cols], dst, gsem.at[slot, i]).start()

    def hidden(t0, nt, g0, g1):
        tile(t0, 0, "start")

        def body(i, _):
            slot = i % 2

            @pl.when(i + 1 < nt)
            def _():
                tile(t0 + i + 1, 1 - slot, "start")

            tile(t0 + i, slot, "wait")

            def group(g, _):
                acc = jnp.dot(xa[g], gt[slot], preferred_element_type=F32)
                cols = pl.ds(pl.multiple_of((t0 + i) * TU, TU), TU)
                hid[g, :, cols] = (jax.nn.silu(acc[:, :TU]) * acc[:, TU:]).astype(BF16)
                return 0

            lax.fori_loop(g0, g1, group, 0)
            return 0

        lax.fori_loop(0, nt, body, 0)

    got("ax")
    start("r1x", "l1x")
    got("r1")
    start("d2p")
    got("l1")
    start("d2m")
    got("r1x")
    start("d2xp")
    got("l1x")
    start("d2xm")
    mine.wait()
    got("mg", "mu")
    hidden(0, 2 * per, 0, 3)
    got("ng0", "ng1")
    start("qg0", "qg1")
    got("d2p", "d2m", "d2xp", "d2xm")
    hidden(0, 2 * per, 3, 4)
    got("nu0", "nu1")
    start("qu0", "qu1")
    got("qg0", "qg1", "qu0", "qu1")
    hidden(2 * per, 2 * per, 0, 4)
    got("nd00", "nd10")
    start("qd00", "qd10")
    got("nd01", "nd11")
    start("qd01", "qd11")
    got("md", "qd00", "qd10", "qd01", "qd11")

    def wtile(s, j, act):
        slot = j % 2
        cols = pl.ds(pl.multiple_of(j * CW, CW), CW)
        for i in range(4):
            src = wd_ref.at[:, cols] if i == 0 else D.at[i - 1, :, cols]
            c = pltpu.make_async_copy(src, wt.at[s, slot, pl.ds(i * units, units)], wsem.at[s, slot, i])
            c.start() if act == "start" else c.wait()

    for s in range(3):
        wtile(s, 0, "start")

    def term(s, g, j):
        @pl.when(j + 1 < NJ)
        def _():
            wtile(s, j + 1, "start")

        wtile(s, j, "wait")

    def far(j, i):
        to = YP if i == 0 else YM
        return remote(sf.at[j % 2, i], rf.at[i, j], fs.at[j % 2, i], fr.at[i, j], to)

    def near(j, i):
        to = YP if i == 0 else YM
        return remote(sn.at[j % 2, i], rn.at[i, j], ns.at[j % 2, i], nr.at[i, j], to)

    def across(j):
        return remote(sx.at[j % 2], rx.at[j], xs.at[j % 2], xr.at[j], X2)

    def store(j):
        cols = pl.ds(pl.multiple_of(j * CW, CW), CW)
        return pltpu.make_async_copy(yo.at[j % 2], y_ref.at[:, cols], ysem.at[j % 2])

    def step(i, _):
        @pl.when(i < NJ)
        def _():
            j = i
            slot = j % 2
            term(0, 3, j)
            acc = jnp.dot(hid[3], wt[0, slot], preferred_element_type=F32).astype(BF16)

            @pl.when(j >= 2)
            def _():
                far(j - 2, 0).wait_send()
                far(j - 2, 1).wait_send()

            for a in range(2):
                for b in range(2):
                    sf[slot, a, b] = acc[b * R + a * h:b * R + (a + 1) * h]
            far(j, 0).start()
            far(j, 1).start()

        @pl.when(jnp.logical_and(i >= 1, i < NJ + 1))
        def _():
            j = i - 1
            slot = j % 2
            term(1, 1, j)
            a2 = jnp.dot(hid[2], wt[1, slot], preferred_element_type=F32)
            a1 = jnp.dot(hid[1], wt[1, slot], preferred_element_type=F32)

            @pl.when(j >= 2)
            def _():
                near(j - 2, 0).wait_send()
                near(j - 2, 1).wait_send()

            far(j, 0).wait_recv()
            for b in range(2):
                sn[slot, 0, b * R:b * R + h] = (a2[b * R:b * R + h] + rf[0, j, b].astype(F32)).astype(BF16)
                sn[slot, 0, b * R + h:(b + 1) * R] = a2[b * R + h:(b + 1) * R].astype(BF16)
            near(j, 0).start()
            far(j, 1).wait_recv()
            for b in range(2):
                sn[slot, 1, b * R:b * R + h] = a1[b * R:b * R + h].astype(BF16)
                sn[slot, 1, b * R + h:(b + 1) * R] = (a1[b * R + h:(b + 1) * R] + rf[1, j, b].astype(F32)).astype(BF16)
            near(j, 1).start()

        @pl.when(jnp.logical_and(i >= 2, i < NJ + 2))
        def _():
            j = i - 2
            slot = j % 2
            term(2, 0, j)
            acc = jnp.dot(hid[0], wt[2, slot], preferred_element_type=F32)

            @pl.when(j >= 2)
            def _():
                across(j - 2).wait_send()

            near(j, 0).wait_recv()
            near(j, 1).wait_recv()
            acc = acc + rn[0, j].astype(F32) + rn[1, j].astype(F32)
            own[slot] = acc[:R]
            sx[slot] = acc[R:].astype(BF16)
            across(j).start()

        @pl.when(i >= 3)
        def _():
            j = i - 3
            slot = j % 2

            @pl.when(j >= 2)
            def _():
                store(j - 2).wait()

            across(j).wait_recv()
            yo[slot] = (own[slot] + rx[j].astype(F32)).astype(BF16)
            store(j).start()

        return 0

    lax.fori_loop(0, NJ + 3, step, 0)
    for j in (NJ - 2, NJ - 1):
        for i in range(2):
            far(j, i).wait_send()
            near(j, i).wait_send()
        across(j).wait_send()
        store(j).wait()
    for a in jobs.values():
        a.wait_send()


def solution(mesh):
    side = math.isqrt(mesh.shape["tp"] // 2)

    def step(x, wg, wu, wd):
        R, d = x.shape
        h = R // 2
        units = wg.shape[1]
        NJ = d // CW
        hbm = pl.BlockSpec(memory_space=pltpu.HBM)
        dma = pltpu.SemaphoreType.DMA
        n_jobs = 28
        out = pl.pallas_call(
            functools.partial(kernel, side),
            name="mlp_ring",
            out_shape=[
                jax.ShapeDtypeStruct((R, d), BF16),
                jax.ShapeDtypeStruct((3, d, units), BF16),
                jax.ShapeDtypeStruct((3, d, units), BF16),
                jax.ShapeDtypeStruct((3, units, d), BF16),
            ],
            in_specs=[hbm] * 4,
            out_specs=[hbm] * 4,
            scratch_shapes=[
                pltpu.VMEM((4, 2 * R, d), BF16),
                pltpu.VMEM((4, 2 * R, 4 * units), BF16),
                pltpu.VMEM((2, NJ, 2, h, CW), BF16),
                pltpu.VMEM((2, NJ, 2 * R, CW), BF16),
                pltpu.VMEM((NJ, R, CW), BF16),
                pltpu.VMEM((2, d, 2 * TU), BF16),
                pltpu.VMEM((3, 2, 4 * units, CW), BF16),
                pltpu.VMEM((2, 2, 2, h, CW), BF16),
                pltpu.VMEM((2, 2, 2 * R, CW), BF16),
                pltpu.VMEM((2, R, CW), BF16),
                pltpu.VMEM((2, R, CW), F32),
                pltpu.VMEM((2, R, CW), BF16),
                dma((n_jobs,)), dma((n_jobs,)), dma, dma((2, 2)), dma((3, 2, 4)),
                dma((2, 2)), dma((2, NJ)), dma((2, 2)), dma((2, NJ)), dma((2,)), dma((NJ,)), dma((2,)),
            ],
            compiler_params=pltpu.CompilerParams(
                collective_id=0, has_side_effects=True, vmem_limit_bytes=67043328),
        )(x, wg, wu, wd)
        return out[0]

    return jax.shard_map(
        step,
        mesh=mesh,
        in_specs=(P(("dp", "tp"), None), P(None, "tp"), P(None, "tp"), P("tp", None)),
        out_specs=P(("dp", "tp"), None),
        check_vma=False,
    )
```

time: 679 us -> 394 us (0.58)
  waiting for transfers between devices: 522 us -> 0 us
  Pallas kernels: 0 us -> 387 us
  matrix products: 144 us -> 0 us
  between operations: 13.4 us -> 0.01 us
    pallas_call x0 -> x1, Pallas kernels: none -> 387 us  [step(): pl.pallas_call(functools.partial(kernel, side), name='mlp_ring', out_shap...]
    unnamed x3 -> x0, waiting for transfers between devices: 303 us -> none
    all_gather x1 -> x0, waiting for transfers between devices: 219 us -> none  [step(): rows = lax.all_gather(x, 'tp', axis=0, tiled=True)]
    dot_general x3 -> x0, matrix products: 144 us -> none  [the longest x1 51.3 us: step(): up = jnp.dot(rows, w_up, preferred_element_type=jnp.float32)]
  transfers between devices with their start and end apart: 2 -> 0, of which waited for: 2 -> 0; matrix products, arithmetic and copies ran while one was open for 0% -> 0% of each run, Pallas kernels for 0% -> 0%
where the time goes in v1:
time: 394 us; the launch traced here: 391 us
  Pallas kernels  387 us (98%)
    pallas_call x1, Pallas kernels, step(): pl.pallas_call(functools.partial(kernel, side), name='mlp_ring', out_shap...  387 us

profile of v1, /device:TPU:97, one launch (start us, length us, event | category | flops | bytes accessed | tf_op | source)
XLA Modules:
  0.0 390.6 jit_solution(10920596081690312363)
XLA Ops:
  0.0 387.4 %mlp_ring.1 = (bf16[224,5120]{1,0:T(8,128)(2,1)}, bf16[3,5120,512]{2,1,0:T(8,128)(2,1)}, bf16[3,5120,512]{2,1,0:T(8,128)(2,1)}, bf16[3,512,5120]{2,1,0:T(8,128)(2,1)}) custom-call(bf16[224,5120]{1,0:T(8,128)(2,1)} %x_ref.1, bf16[5120,512]{1,0:T(8,128)(2,1)} %wg_ref.1, bf16[5120,512]{1,0:T(8,128)(2,1)} %wu_ref.1, bf16[512,5120]{1,0:T(8,128)(2,1)} %wd_ref.1), custom_call_target="tpu_custom_call" | custom-call | tf_op jit(solution)/shard_map/mlp_ring/pallas_call | solution.py:286
  387.4 3.2 copy.6

commit v2 on v1

v2 whole, which is shorter than its diff:
```python
import functools
import math

import jax
import jax.numpy as jnp
from jax import lax
from jax.experimental import pallas as pl
from jax.experimental.pallas import tpu as pltpu
from jax.sharding import PartitionSpec as P

MESH = pl.DeviceIdType.MESH
F32, BF16 = jnp.float32, jnp.bfloat16
TU = 128
CW = 256
AHEAD = 6
LAG = (5, 7, 10)
SLOTS = 4


def kernel(side, x_ref, wg_ref, wu_ref, wd_ref, y_ref, G, U, D,
           xa, hid, rf, rn, rx, gt, wt, sf, sn, sx, own, yo,
           ssem, rsem, lsem, gsem, wsem, fs, fr, ns, nr, xs, xr, ysem, ds, dr, qs, qr):
    t = lax.axis_index("tp")
    core, row, col = t % 2, (t // 2) % side, t // (2 * side)

    def peer(dx, dy, dc):
        return (((col + dx + side) % side) * side + (row + dy + side) % side) * 2 + (core + dc) % 2

    XP, XM, X2 = peer(1, 0, 0), peer(-1, 0, 0), peer(2, 0, 0)
    YP, YM, CC = peer(0, 1, 0), peer(0, -1, 0), peer(0, 0, 1)

    R, d = x_ref.shape
    h = R // 2
    units = wg_ref.shape[1]
    k = units // 2
    NJ = d // CW

    barrier = pltpu.get_barrier_semaphore()
    for p in (XP, XM, X2, YP, YM, CC):
        pl.semaphore_signal(barrier, inc=1, device_id={"tp": p}, device_id_type=MESH)
    pl.semaphore_wait(barrier, 6)

    def remote(src, dst, s, r, to):
        return pltpu.make_async_remote_copy(
            src_ref=src, dst_ref=dst, send_sem=s, recv_sem=r, device_id={"tp": to}, device_id_type=MESH)

    jobs = {}

    def job(name, src, dst, to):
        i = len(jobs)
        jobs[name] = remote(src, dst, ssem.at[i], rsem.at[i], to)

    job("ax", x_ref, xa.at[0, pl.ds(R, R)], X2)
    job("r1", x_ref, xa.at[1, pl.ds(0, R)], YP)
    job("l1", x_ref, xa.at[2, pl.ds(0, R)], YM)
    job("r1x", xa.at[0, pl.ds(R, R)], xa.at[1, pl.ds(R, R)], YP)
    job("l1x", xa.at[0, pl.ds(R, R)], xa.at[2, pl.ds(R, R)], YM)
    job("d2p", xa.at[1, pl.ds(0, h)], xa.at[3, pl.ds(0, h)], YP)
    job("d2m", xa.at[2, pl.ds(h, h)], xa.at[3, pl.ds(h, h)], YM)
    job("d2xp", xa.at[1, pl.ds(R, h)], xa.at[3, pl.ds(R, h)], YP)
    job("d2xm", xa.at[2, pl.ds(R + h, h)], xa.at[3, pl.ds(R + h, h)], YM)
    job("mg", wg_ref, G.at[0], CC)
    job("mu", wu_ref, U.at[0], CC)
    job("md", wd_ref, D.at[0], CC)
    for i, to in ((0, XP), (1, XM)):
        for q in range(2):
            lo = pl.ds(i * k + q * TU, TU)
            job(f"ng{i}{q}", wg_ref.at[:, lo], G.at[1, :, lo], to)
            job(f"nu{i}{q}", wu_ref.at[:, lo], U.at[1, :, lo], to)
            job(f"qg{i}{q}", G.at[1, :, lo], G.at[2, :, lo], CC)
            job(f"qu{i}{q}", U.at[1, :, lo], U.at[2, :, lo], CC)

    def columns(j):
        return pl.ds(pl.multiple_of(j * CW, CW), CW)

    def down(j, i):
        rows = pl.ds(i * k, k)
        return remote(wd_ref.at[rows, columns(j)], D.at[1, rows, columns(j)], ds.at[j, i], dr.at[j, i], XM if i else XP)

    def pass_on(j):
        return remote(D.at[1, :, columns(j)], D.at[2, :, columns(j)], qs.at[j], qr.at[j], CC)

    def start(*names):
        for a in names:
            jobs[a].start()

    def got(*names):
        for a in names:
            jobs[a].wait_recv()

    mine = pltpu.make_async_copy(x_ref, xa.at[0, pl.ds(0, R)], lsem)
    mine.start()
    start("ax", "r1", "l1", "mg", "mu")
    for q in range(2):
        start(f"ng0{q}", f"ng1{q}", f"nu0{q}", f"nu1{q}")
    start("md")
    for j in range(AHEAD):
        down(j, 0).start()
        down(j, 1).start()

    per = units // TU

    def tile(tt, slot, act):
        kind = tt // per
        cols = pl.ds(pl.multiple_of((tt % per) * TU, TU), TU)
        for i, (w, b) in enumerate(((wg_ref, G), (wu_ref, U))):
            dst = gt.at[slot, :, pl.ds(i * TU, TU)]
            if act == "wait":
                pltpu.make_async_copy(w.at[:, pl.ds(0, TU)], dst, gsem.at[slot, i]).wait()
                continue

            @pl.when(kind == 0)
            def _():
                pltpu.make_async_copy(w.at[:, cols], dst, gsem.at[slot, i]).start()

            @pl.when(kind > 0)
            def _():
                pltpu.make_async_copy(b.at[jnp.maximum(kind - 1, 0), :, cols], dst, gsem.at[slot, i]).start()

    def hidden(t0, by, nt, g0, g1, first=True, then=None):
        if first:
            tile(t0, 0, "start")

        def body(i, _):
            slot = i % 2
            if then is None:
                @pl.when(i + 1 < nt)
                def _():
                    tile(t0 + (i + 1) * by, 1 - slot, "start")
            else:
                tile(jnp.where(i + 1 < nt, t0 + (i + 1) * by, then), 1 - slot, "start")

            tile(t0, slot, "wait")

            def group(g, _):
                acc = jnp.dot(xa[g], gt[slot], preferred_element_type=F32)
                cols = pl.ds(pl.multiple_of((t0 + i * by) * TU, TU), TU)
                hid[g, :, cols] = (jax.nn.silu(acc[:, :TU]) * acc[:, TU:]).astype(BF16)
                return 0

            lax.fori_loop(g0, g1, group, 0)
            return 0

        lax.fori_loop(0, nt, body, 0)

    def swapped(act, q):
        for a in ("g", "u"):
            for i in range(2):
                if act == "take":
                    got(f"n{a}{i}{q}")
                    start(f"q{a}{i}{q}")
                else:
                    got(f"q{a}{i}{q}")

    nb = 2 * per
    got("ax")
    start("r1x", "l1x")
    got("r1")
    start("d2p")
    got("l1")
    start("d2m")
    mine.wait()
    got("mg", "mu")
    hidden(0, 1, nb, 0, 1, then=0)
    got("r1x")
    start("d2xp")
    got("l1x")
    start("d2xm")
    swapped("take", 0)
    hidden(0, 1, nb, 1, 3, first=False, then=nb)
    swapped("wait", 0)
    hidden(nb, 2, per, 0, 3, first=False, then=0)
    got("d2p", "d2m", "d2xp", "d2xm")
    hidden(0, 1, nb, 3, 4, first=False, then=nb)
    hidden(nb, 2, per, 3, 4, first=False)
    swapped("take", 1)
    hidden(nb + 1, 2, per // 2, 3, 4, then=nb + 1)
    hidden(nb + 1, 2, per // 2, 1, 3, first=False)
    swapped("wait", 1)
    hidden(nb + 1 + per, 2, per // 2, 3, 4, then=nb + 1 + per)

    def wtile(s, j, act):
        slot = j % 2
        cols = pl.ds(pl.multiple_of(j * CW, CW), CW)
        for i in range(4):
            src = wd_ref.at[:, cols] if i == 0 else D.at[i - 1, :, cols]
            c = pltpu.make_async_copy(src, wt.at[s, slot, pl.ds(i * units, units)], wsem.at[s, slot, i])
            c.start() if act == "start" else c.wait()

    def take_down(j):
        down(j, 0).wait_recv()
        down(j, 1).wait_recv()
        pass_on(j).start()

    def term(s, j):
        wtile(s, j, "wait")

        @pl.when(j + 1 < NJ)
        def _():
            wtile(s, j + 1, "start")

    def far(j, i):
        to = YP if i == 0 else YM
        return remote(sf.at[j % SLOTS, i], rf.at[i, j], fs.at[j % SLOTS, i], fr.at[i, j], to)

    def near(j, i):
        to = YP if i == 0 else YM
        return remote(sn.at[j % SLOTS, i], rn.at[i, j], ns.at[j % SLOTS, i], nr.at[i, j], to)

    def across(j):
        return remote(sx.at[j % SLOTS], rx.at[j], xs.at[j % SLOTS], xr.at[j], X2)

    def store(j):
        cols = pl.ds(pl.multiple_of(j * CW, CW), CW)
        return pltpu.make_async_copy(yo.at[j % 2], y_ref.at[:, cols], ysem.at[j % 2])

    def far_step(j):
        slot = j % SLOTS
        wtile(0, j, "wait")
        acc = jnp.dot(hid[3], wt[0, j % 2], preferred_element_type=F32).astype(BF16)

        @pl.when(j >= SLOTS)
        def _():
            far(j - SLOTS, 0).wait_send()
            far(j - SLOTS, 1).wait_send()

        for a in range(2):
            for b in range(2):
                sf[slot, a, b] = acc[b * R + a * h:b * R + (a + 1) * h]
        far(j, 0).start()
        far(j, 1).start()

        @pl.when(j + 1 < NJ)
        def _():
            pass_on(j + 1).wait_recv()
            wtile(0, j + 1, "start")

        @pl.when(j + 2 < NJ)
        def _():
            take_down(j + 2)

        @pl.when(j + AHEAD < NJ)
        def _():
            down(j + AHEAD, 0).start()
            down(j + AHEAD, 1).start()

    def near_step(j):
        slot = j % SLOTS
        term(1, j)
        a2 = jnp.dot(hid[2], wt[1, j % 2], preferred_element_type=F32)
        a1 = jnp.dot(hid[1], wt[1, j % 2], preferred_element_type=F32)

        @pl.when(j >= SLOTS)
        def _():
            near(j - SLOTS, 0).wait_send()
            near(j - SLOTS, 1).wait_send()

        far(j, 0).wait_recv()
        for b in range(2):
            sn[slot, 0, b * R:b * R + h] = (a2[b * R:b * R + h] + rf[0, j, b].astype(F32)).astype(BF16)
            sn[slot, 0, b * R + h:(b + 1) * R] = a2[b * R + h:(b + 1) * R].astype(BF16)
        near(j, 0).start()
        far(j, 1).wait_recv()
        for b in range(2):
            sn[slot, 1, b * R:b * R + h] = a1[b * R:b * R + h].astype(BF16)
            sn[slot, 1, b * R + h:(b + 1) * R] = (a1[b * R + h:(b + 1) * R] + rf[1, j, b].astype(F32)).astype(BF16)
        near(j, 1).start()

    def own_step(j):
        slot = j % SLOTS
        term(2, j)
        acc = jnp.dot(hid[0], wt[2, j % 2], preferred_element_type=F32)

        @pl.when(j >= SLOTS)
        def _():
            across(j - SLOTS).wait_send()

        near(j, 0).wait_recv()
        near(j, 1).wait_recv()
        acc = acc + rn[0, j].astype(F32) + rn[1, j].astype(F32)
        own[slot] = acc[:R]
        sx[slot] = acc[R:].astype(BF16)
        across(j).start()

    def last_step(j):
        @pl.when(j >= 2)
        def _():
            store(j - 2).wait()

        across(j).wait_recv()
        yo[j % 2] = (own[j % SLOTS] + rx[j].astype(F32)).astype(BF16)
        store(j).start()

    def loop(lo, hi, f):
        def body(i, _):
            f(i)
            return 0

        lax.fori_loop(lo, hi, body, 0)

    got("md")
    take_down(0)
    pass_on(0).wait_recv()
    for s in range(3):
        wtile(s, 0, "start")
    take_down(1)
    loop(0, 2, far_step)
    hidden(nb + 1 + per, 2, per // 2, 1, 3, first=False, then=nb + 1)
    loop(2, LAG[0], far_step)
    hidden(nb + 1, 2, per, 0, 1, first=False)

    def step(i):
        @pl.when(i < NJ)
        def _():
            far_step(i)

        @pl.when(i < NJ + LAG[0])
        def _():
            near_step(i - LAG[0])

        @pl.when(jnp.logical_and(i >= LAG[1], i < NJ + LAG[1]))
        def _():
            own_step(i - LAG[1])

        @pl.when(i >= LAG[2])
        def _():
            last_step(i - LAG[2])

    loop(LAG[0], NJ + LAG[2], step)
    for j in range(NJ - SLOTS, NJ):
        for i in range(2):
            far(j, i).wait_send()
            near(j, i).wait_send()
        across(j).wait_send()
    store(NJ - 2).wait()
    store(NJ - 1).wait()

    def sent(j):
        down(j, 0).wait_send()
        down(j, 1).wait_send()
        pass_on(j).wait_send()

    loop(0, NJ, sent)
    for a in jobs.values():
        a.wait_send()


def solution(mesh):
    side = math.isqrt(mesh.shape["tp"] // 2)

    def step(x, wg, wu, wd):
        R, d = x.shape
        h = R // 2
        units = wg.shape[1]
        NJ = d // CW
        hbm = pl.BlockSpec(memory_space=pltpu.HBM)
        dma = pltpu.SemaphoreType.DMA
        n_jobs = 28
        out = pl.pallas_call(
            functools.partial(kernel, side),
            name="mlp_ring",
            out_shape=[
                jax.ShapeDtypeStruct((R, d), BF16),
                jax.ShapeDtypeStruct((3, d, units), BF16),
                jax.ShapeDtypeStruct((3, d, units), BF16),
                jax.ShapeDtypeStruct((3, units, d), BF16),
            ],
            in_specs=[hbm] * 4,
            out_specs=[hbm] * 4,
            scratch_shapes=[
                pltpu.VMEM((4, 2 * R, d), BF16),
                pltpu.VMEM((4, 2 * R, 4 * units), BF16),
                pltpu.VMEM((2, NJ, 2, h, CW), BF16),
                pltpu.VMEM((2, NJ, 2 * R, CW), BF16),
                pltpu.VMEM((NJ, R, CW), BF16),
                pltpu.VMEM((2, d, 2 * TU), BF16),
                pltpu.VMEM((3, 2, 4 * units, CW), BF16),
                pltpu.VMEM((SLOTS, 2, 2, h, CW), BF16),
                pltpu.VMEM((SLOTS, 2, 2 * R, CW), BF16),
                pltpu.VMEM((SLOTS, R, CW), BF16),
                pltpu.VMEM((SLOTS, R, CW), F32),
                pltpu.VMEM((2, R, CW), BF16),
                dma((n_jobs,)), dma((n_jobs,)), dma, dma((2, 2)), dma((3, 2, 4)),
                dma((SLOTS, 2)), dma((2, NJ)), dma((SLOTS, 2)), dma((2, NJ)), dma((SLOTS,)), dma((NJ,)), dma((2,)),
                dma((NJ, 2)), dma((NJ, 2)), dma((NJ,)), dma((NJ,)),
            ],
            compiler_params=pltpu.CompilerParams(
                collective_id=0, has_side_effects=True, vmem_limit_bytes=67043328),
        )(x, wg, wu, wd)
        return out[0]

    return jax.shard_map(
        step,
        mesh=mesh,
        in_specs=(P(("dp", "tp"), None), P(None, "tp"), P(None, "tp"), P("tp", None)),
        out_specs=P(("dp", "tp"), None),
        check_vma=False,
    )
```

time: 394 us -> 364 us (0.924)
  Pallas kernels: 387 us -> 360 us
    pallas_call x1, Pallas kernels: 387 us -> 360 us  [step(): pl.pallas_call(functools.partial(kernel, side), name='mlp_ring', out_shap...]
where the time goes in v2:
time: 364 us; the launch traced here: 363 us
  Pallas kernels  360 us (99%)
    pallas_call x1, Pallas kernels, step(): pl.pallas_call(functools.partial(kernel, side), name='mlp_ring', out_shap...  360 us

profile of v2, /device:TPU:97, one launch (start us, length us, event | category | flops | bytes accessed | tf_op | source)
XLA Modules:
  0.0 363.3 jit_solution(7809713894381891210)
XLA Ops:
  0.0 360.1 %mlp_ring.1 = (bf16[224,5120]{1,0:T(8,128)(2,1)}, bf16[3,5120,512]{2,1,0:T(8,128)(2,1)}, bf16[3,5120,512]{2,1,0:T(8,128)(2,1)}, bf16[3,512,5120]{2,1,0:T(8,128)(2,1)}) custom-call(bf16[224,5120]{1,0:T(8,128)(2,1)} %x_ref.1, bf16[5120,512]{1,0:T(8,128)(2,1)} %wg_ref.1, bf16[5120,512]{1,0:T(8,128)(2,1)} %wu_ref.1, bf16[512,5120]{1,0:T(8,128)(2,1)} %wd_ref.1), custom_call_target="tpu_custom_call" | custom-call | tf_op jit(solution)/shard_map/mlp_ring/pallas_call | solution.py:359
  360.1 3.2 copy.6

commit v3 on v2

--- a/solution.py
+++ b/solution.py
@@ -12,14 +12,17 @@
 F32, BF16 = jnp.float32, jnp.bfloat16
 TU = 128
 CW = 256
-AHEAD = 6
-LAG = (5, 7, 10)
+AHEAD = 9
+LAG = (5, 7, 12)
 SLOTS = 4
+CROSS = 3
+WIDE = 6
 
 
 def kernel(side, x_ref, wg_ref, wu_ref, wd_ref, y_ref, G, U, D,
            xa, hid, rf, rn, rx, gt, wt, sf, sn, sx, own, yo,
-           ssem, rsem, lsem, gsem, wsem, fs, fr, ns, nr, xs, xr, ysem, ds, dr, qs, qr):
+           ssem, rsem, lsem, gsem, wsem, fs, fr, ns, nr, xs, xr, ysem, ds, dr, qs, qr,
+           wx, so, ro, xsem, os, orr):
     t = lax.axis_index("tp")
     core, row, col = t % 2, (t // 2) % side, t // (2 * side)
 
@@ -34,6 +37,7 @@
     units = wg_ref.shape[1]
     k = units // 2
     NJ = d // CW
+    N0 = NJ - CROSS
 
     barrier = pltpu.get_barrier_semaphore()
     for p in (XP, XM, X2, YP, YM, CC):
@@ -166,14 +170,18 @@
     start("d2xp")
     got("l1x")
     start("d2xm")
+    hidden(0, 1, nb, 1, 3, first=False)
     swapped("take", 0)
-    hidden(0, 1, nb, 1, 3, first=False, then=nb)
+    hidden(nb, 2, per // 2, 0, 3)
     swapped("wait", 0)
-    hidden(nb, 2, per, 0, 3, first=False, then=0)
+    hidden(nb + per, 2, per // 2, 0, 3, then=0)
+    got("ng01", "ng11")
+    start("qg01", "qg11")
     got("d2p", "d2m", "d2xp", "d2xm")
     hidden(0, 1, nb, 3, 4, first=False, then=nb)
     hidden(nb, 2, per, 3, 4, first=False)
-    swapped("take", 1)
+    got("nu01", "nu11")
+    start("qu01", "qu11")
     hidden(nb + 1, 2, per // 2, 3, 4, then=nb + 1)
     hidden(nb + 1, 2, per // 2, 1, 3, first=False)
     swapped("wait", 1)
@@ -199,96 +207,184 @@
         def _():
             wtile(s, j + 1, "start")
 
-    def far(j, i):
+    def far(j, i, half=False):
         to = YP if i == 0 else YM
-        return remote(sf.at[j % SLOTS, i], rf.at[i, j], fs.at[j % SLOTS, i], fr.at[i, j], to)
-
-    def near(j, i):
+        a, b = (sf.at[j % SLOTS, i, 0], rf.at[i, j, 0]) if half else (sf.at[j % SLOTS, i], rf.at[i, j])
+        return remote(a, b, fs.at[j % SLOTS, i], fr.at[i, j], to)
+
+    def near(j, i, half=False):
         to = YP if i == 0 else YM
-        return remote(sn.at[j % SLOTS, i], rn.at[i, j], ns.at[j % SLOTS, i], nr.at[i, j], to)
+        a, b = sn.at[j % SLOTS, i], rn.at[i, j]
+        if half:
+            a, b = a.at[pl.ds(0, R)], b.at[pl.ds(0, R)]
+        return remote(a, b, ns.at[j % SLOTS, i], nr.at[i, j], to)
+
+    def settle(what, j):
+        for half, these in ((False, j < N0), (True, j >= N0)):
+            @pl.when(these)
+            def _():
+                what(j, 0, half).wait_send()
+                what(j, 1, half).wait_send()
 
     def across(j):
-        return remote(sx.at[j % SLOTS], rx.at[j], xs.at[j % SLOTS], xr.at[j], X2)
+        return remote(sx.at[j % WIDE], rx.at[j], xs.at[j % WIDE], xr.at[j], X2)
 
     def store(j):
         cols = pl.ds(pl.multiple_of(j * CW, CW), CW)
         return pltpu.make_async_copy(yo.at[j % 2], y_ref.at[:, cols], ysem.at[j % 2])
 
+    def over(j):
+        return remote(so.at[j % 2], ro.at[j - N0], os.at[j % 2], orr.at[j - N0], X2)
+
+    def xtile(j, act):
+        for i in range(4):
+            src = wd_ref.at[:, columns(j)] if i == 0 else D.at[i - 1, :, columns(j)]
+            c = pltpu.make_async_copy(src, wx.at[pl.ds(i * units, units)], xsem.at[i])
+            c.start() if act == "start" else c.wait()
+
+    def over_step(j):
+        @pl.when(j >= N0 + 2)
+        def _():
+            over(j - 2).wait_send()
+
+        xtile(j, "wait")
+
+        def group(g, _):
+            so[j % 2, g] = jnp.dot(hid[g, R:], wx[...], preferred_element_type=F32).astype(BF16)
+            return 0
+
+        lax.fori_loop(0, 4, group, 0)
+        over(j).start()
+
     def far_step(j):
         slot = j % SLOTS
         wtile(0, j, "wait")
-        acc = jnp.dot(hid[3], wt[0, j % 2], preferred_element_type=F32).astype(BF16)
 
         @pl.when(j >= SLOTS)
         def _():
-            far(j - SLOTS, 0).wait_send()
-            far(j - SLOTS, 1).wait_send()
-
-        for a in range(2):
-            for b in range(2):
-                sf[slot, a, b] = acc[b * R + a * h:b * R + (a + 1) * h]
-        far(j, 0).start()
-        far(j, 1).start()
+            settle(far, j - SLOTS)
+
+        @pl.when(j < N0)
+        def _():
+            acc = jnp.dot(hid[3], wt[0, j % 2], preferred_element_type=F32).astype(BF16)
+            for a in range(2):
+                for b in range(2):
+                    sf[slot, a, b] = acc[b * R + a * h:b * R + (a + 1) * h]
+            far(j, 0).start()
+            far(j, 1).start()
+
+        @pl.when(j >= N0)
+        def _():
+            acc = jnp.dot(hid[3, :R], wt[0, j % 2], preferred_element_type=F32)
+            over(j).wait_recv()
+            acc = (acc + ro[jnp.maximum(j - N0, 0), 3].astype(F32)).astype(BF16)
+            for a in range(2):
+                sf[slot, a, 0] = acc[a * h:(a + 1) * h]
+                far(j, a, True).start()
+
+        @pl.when(j + 1 < N0)
+        def _():
+            pass_on(j + 1).wait_recv()
 
         @pl.when(j + 1 < NJ)
         def _():
-            pass_on(j + 1).wait_recv()
             wtile(0, j + 1, "start")
 
-        @pl.when(j + 2 < NJ)
+        @pl.when(j + 2 < N0)
         def _():
             take_down(j + 2)
 
-        @pl.when(j + AHEAD < NJ)
+        @pl.when(j + AHEAD < N0)
         def _():
             down(j + AHEAD, 0).start()
             down(j + AHEAD, 1).start()
+
+        @pl.when(j < NJ - N0)
+        def _():
+            down(j + N0, 0).start()
+            down(j + N0, 1).start()
+
+        @pl.when(jnp.logical_and(j % 2 == 0, jnp.logical_and(j >= 4, j < 4 + 2 * (NJ - N0))))
+        def _():
+            take_down(N0 + (j - 4) // 2)
 
     def near_step(j):
         slot = j % SLOTS
         term(1, j)
-        a2 = jnp.dot(hid[2], wt[1, j % 2], preferred_element_type=F32)
-        a1 = jnp.dot(hid[1], wt[1, j % 2], preferred_element_type=F32)
-
         @pl.when(j >= SLOTS)
         def _():
-            near(j - SLOTS, 0).wait_send()
-            near(j - SLOTS, 1).wait_send()
-
-        far(j, 0).wait_recv()
-        for b in range(2):
-            sn[slot, 0, b * R:b * R + h] = (a2[b * R:b * R + h] + rf[0, j, b].astype(F32)).astype(BF16)
-            sn[slot, 0, b * R + h:(b + 1) * R] = a2[b * R + h:(b + 1) * R].astype(BF16)
-        near(j, 0).start()
-        far(j, 1).wait_recv()
-        for b in range(2):
-            sn[slot, 1, b * R:b * R + h] = a1[b * R:b * R + h].astype(BF16)
-            sn[slot, 1, b * R + h:(b + 1) * R] = (a1[b * R + h:(b + 1) * R] + rf[1, j, b].astype(F32)).astype(BF16)
-        near(j, 1).start()
+            settle(near, j - SLOTS)
+
+        @pl.when(j < N0)
+        def _():
+            a2 = jnp.dot(hid[2], wt[1, j % 2], preferred_element_type=F32)
+            a1 = jnp.dot(hid[1], wt[1, j % 2], preferred_element_type=F32)
+            far(j, 0).wait_recv()
+            for b in range(2):
+                sn[slot, 0, b * R:b * R + h] = (a2[b * R:b * R + h] + rf[0, j, b].astype(F32)).astype(BF16)
+                sn[slot, 0, b * R + h:(b + 1) * R] = a2[b * R + h:(b + 1) * R].astype(BF16)
+            near(j, 0).start()
+            far(j, 1).wait_recv()
+            for b in range(2):
+                sn[slot, 1, b * R:b * R + h] = a1[b * R:b * R + h].astype(BF16)
+                sn[slot, 1, b * R + h:(b + 1) * R] = (a1[b * R + h:(b + 1) * R] + rf[1, j, b].astype(F32)).astype(BF16)
+            near(j, 1).start()
+
+        @pl.when(j >= N0)
+        def _():
+            o = jnp.maximum(j - N0, 0)
+            a2 = jnp.dot(hid[2, :R], wt[1, j % 2], preferred_element_type=F32) + ro[o, 2].astype(F32)
+            a1 = jnp.dot(hid[1, :R], wt[1, j % 2], preferred_element_type=F32) + ro[o, 1].astype(F32)
+            far(j, 0, True).wait_recv()
+            sn[slot, 0, :h] = (a2[:h] + rf[0, j, 0].astype(F32)).astype(BF16)
+            sn[slot, 0, h:R] = a2[h:].astype(BF16)
+            near(j, 0, True).start()
+            far(j, 1, True).wait_recv()
+            sn[slot, 1, :h] = a1[:h].astype(BF16)
+            sn[slot, 1, h:R] = (a1[h:] + rf[1, j, 0].astype(F32)).astype(BF16)
+            near(j, 1, True).start()
 
     def own_step(j):
-        slot = j % SLOTS
+        slot = j % WIDE
         term(2, j)
-        acc = jnp.dot(hid[0], wt[2, j % 2], preferred_element_type=F32)
-
-        @pl.when(j >= SLOTS)
-        def _():
-            across(j - SLOTS).wait_send()
-
-        near(j, 0).wait_recv()
-        near(j, 1).wait_recv()
-        acc = acc + rn[0, j].astype(F32) + rn[1, j].astype(F32)
-        own[slot] = acc[:R]
-        sx[slot] = acc[R:].astype(BF16)
-        across(j).start()
+
+        @pl.when(j < N0)
+        def _():
+            acc = jnp.dot(hid[0], wt[2, j % 2], preferred_element_type=F32)
+
+            @pl.when(j >= WIDE)
+            def _():
+                across(j - WIDE).wait_send()
+
+            near(j, 0).wait_recv()
+            near(j, 1).wait_recv()
+            acc = acc + rn[0, j].astype(F32) + rn[1, j].astype(F32)
+            own[slot] = acc[:R]
+            sx[slot] = acc[R:].astype(BF16)
+            across(j).start()
+
+        @pl.when(j >= N0)
+        def _():
+            acc = jnp.dot(hid[0, :R], wt[2, j % 2], preferred_element_type=F32)
+            acc = acc + ro[jnp.maximum(j - N0, 0), 0].astype(F32)
+            near(j, 0, True).wait_recv()
+            near(j, 1, True).wait_recv()
+            own[slot] = acc + rn[0, j, :R].astype(F32) + rn[1, j, :R].astype(F32)
 
     def last_step(j):
         @pl.when(j >= 2)
         def _():
             store(j - 2).wait()
 
-        across(j).wait_recv()
-        yo[j % 2] = (own[j % SLOTS] + rx[j].astype(F32)).astype(BF16)
+        @pl.when(j < N0)
+        def _():
+            across(j).wait_recv()
+            yo[j % 2] = (own[j % WIDE] + rx[j].astype(F32)).astype(BF16)
+
+        @pl.when(j >= N0)
+        def _():
+            yo[j % 2] = own[j % WIDE].astype(BF16)
+
         store(j).start()
 
     def loop(lo, hi, f):
@@ -310,6 +406,14 @@
     hidden(nb + 1, 2, per, 0, 1, first=False)
 
     def step(i):
+        crossing = jnp.logical_and(i % 2 == 1, i < 5 + 2 * (NJ - N0))
+        o = N0 + (i - 5) // 2
+
+        @pl.when(crossing)
+        def _():
+            pass_on(o).wait_recv()
+            xtile(o, "start")
+
         @pl.when(i < NJ)
         def _():
             far_step(i)
@@ -325,13 +429,20 @@
         @pl.when(i >= LAG[2])
         def _():
             last_step(i - LAG[2])
+
+        @pl.when(crossing)
+        def _():
+            over_step(o)
 
     loop(LAG[0], NJ + LAG[2], step)
     for j in range(NJ - SLOTS, NJ):
         for i in range(2):
-            far(j, i).wait_send()
-            near(j, i).wait_send()
+            far(j, i, j >= N0).wait_send()
+            near(j, i, j >= N0).wait_send()
+    for j in range(N0 - WIDE, N0):
         across(j).wait_send()
+    over(NJ - 2).wait_send()
+    over(NJ - 1).wait_send()
     store(NJ - 2).wait()
     store(NJ - 1).wait()
 
@@ -377,12 +488,16 @@
                 pltpu.VMEM((3, 2, 4 * units, CW), BF16),
                 pltpu.VMEM((SLOTS, 2, 2, h, CW), BF16),
                 pltpu.VMEM((SLOTS, 2, 2 * R, CW), BF16),
-                pltpu.VMEM((SLOTS, R, CW), BF16),
-                pltpu.VMEM((SLOTS, R, CW), F32),
+                pltpu.VMEM((WIDE, R, CW), BF16),
+                pltpu.VMEM((WIDE, R, CW), F32),
                 pltpu.VMEM((2, R, CW), BF16),
                 dma((n_jobs,)), dma((n_jobs,)), dma, dma((2, 2)), dma((3, 2, 4)),
-                dma((SLOTS, 2)), dma((2, NJ)), dma((SLOTS, 2)), dma((2, NJ)), dma((SLOTS,)), dma((NJ,)), dma((2,)),
+                dma((SLOTS, 2)), dma((2, NJ)), dma((SLOTS, 2)), dma((2, NJ)), dma((WIDE,)), dma((NJ,)), dma((2,)),
                 dma((NJ, 2)), dma((NJ, 2)), dma((NJ,)), dma((NJ,)),
+                pltpu.VMEM((4 * units, CW), BF16),
+                pltpu.VMEM((2, 4, R, CW), BF16),
+                pltpu.VMEM((CROSS, 4, R, CW), BF16),
+                dma((4,)), dma((2,)), dma((CROSS,)),
             ],
             compiler_params=pltpu.CompilerParams(
                 collective_id=0, has_side_effects=True, vmem_limit_bytes=67043328),

time: 364 us -> 351 us (0.964)
  Pallas kernels: 360 us -> 347 us
    pallas_call x1, Pallas kernels: 360 us -> 347 us  [step(): pl.pallas_call(functools.partial(kernel, side), name='mlp_ring', out_shap...]
where the time goes in v3:
time: 351 us; the launch traced here: 350 us
  Pallas kernels  347 us (99%)
    pallas_call x1, Pallas kernels, step(): pl.pallas_call(functools.partial(kernel, side), name='mlp_ring', out_shap...  347 us

profile of v3, /device:TPU:97, one launch (start us, length us, event | category | flops | bytes accessed | tf_op | source)
XLA Modules:
  0.0 349.7 jit_solution(6989087527819782125)
XLA Ops:
  0.0 346.5 %mlp_ring.1 = (bf16[224,5120]{1,0:T(8,128)(2,1)}, bf16[3,5120,512]{2,1,0:T(8,128)(2,1)}, bf16[3,5120,512]{2,1,0:T(8,128)(2,1)}, bf16[3,512,5120]{2,1,0:T(8,128)(2,1)}) custom-call(bf16[224,5120]{1,0:T(8,128)(2,1)} %x_ref.1, bf16[5120,512]{1,0:T(8,128)(2,1)} %wg_ref.1, bf16[5120,512]{1,0:T(8,128)(2,1)} %wu_ref.1, bf16[512,5120]{1,0:T(8,128)(2,1)} %wd_ref.1), custom_call_target="tpu_custom_call" | custom-call | tf_op jit(solution)/shard_map/mlp_ring/pallas_call | solution.py:470
  346.6 3.2 copy.6
